TPU v7x, 128 devices: a whole 4x4x4 slice. The times are simulated.
128 devices in a mesh: plane: 8 (over z_hi, x), tile: 16 (over z_lo, y, core).
Axes of the slice: x: 4, y: 4, z: 4 (z_hi: 2, z_lo: 2; z = z_hi * 2 + z_lo), core: 2. Of those that a mesh axis runs over, the one named last changes fastest.
Arguments:
- visibility: float32 [2, 262144], P(None, ('plane', 'tile')), may hold values from -6 to 6
- target: int32 [262144, 1], P(('plane', 'tile')), may hold values from 0 to 127; in each aligned block of 2048 rows (0 to 2047, 2048 to 4095, ...) at most 32 rows name the same one
- offset: int32 [262144], P(('plane', 'tile')), may hold values from 0 to 1048575
- taps: float32 [8], replicated, may hold values from 0.1 to 1
- w_plane: float32 [8], P('plane'), may hold values from -300 to 300
Outputs:
- dirty_image: float32 [4096, 4096], P('plane', 'tile')
Inputs may be any that keep to these rules, and one draw needn't show every extreme that they name: `target`: among the rows of one device no value occurs more than 32 times, and some value occurs exactly 32 times.
All inputs are finite; a program needn't handle non-finite values.
Results may differ from a plain program's by a relative error of at most 0.0042.
Values sent between devices are 32-bit elements; how exact they have to be, the bound alone decides.
A program may use at most 128 MiB of HBM per device.

v0:
```python
import math
import jax
import jax.numpy as jnp
from jax import lax
from jax.sharding import Mesh
from jax.sharding import PartitionSpec as P

G = 4096
TILE = ("tile_0", "tile_1", "tile_2")
PLANE = ("plane_0", "plane_1")
PLANE_TILE = ("plane_0", "plane_1", "tile_0", "tile_1", "tile_2")
HIGHEST = lax.Precision.HIGHEST


def split_up(x, dim, length):
    dims = x.shape
    blocks = x.reshape(*dims[:dim], length, dims[dim] // length, *dims[dim + 1 :])
    return jnp.moveaxis(blocks, dim, 0)


def joined_along(blocks, dim):
    blocks = jnp.moveaxis(blocks, 0, dim)
    dims = blocks.shape
    return blocks.reshape(*dims[:dim], dims[dim] * dims[dim + 1], *dims[dim + 2 :])


def moved_by_axis(blocks, axes, sequence):
    dims = [lax.axis_size(a) for a in axes]
    blocks = blocks.reshape(*dims, *blocks.shape[1:])
    for k in sequence:
        blocks = lax.all_to_all(blocks, axes[k], split_axis=k, concat_axis=k, tiled=True)
    return blocks.reshape(-1, *blocks.shape[len(axes) :])


def exchange_by_chip(x, groups, sequence, split_dim, concat_dim):
    length = lax.axis_size(groups[0]) * lax.axis_size(groups[1])
    blocks = split_up(x, split_dim, length)
    return joined_along(moved_by_axis(blocks, groups, sequence), concat_dim)


def shifted(x, axis, by):
    length = lax.axis_size(axis)
    return lax.ppermute(x, axis, [(i, (i + by) % length) for i in range(length)])


def summed_on_arrival(x, axis, dim):
    blocks = split_up(x, dim, lax.axis_size(axis))
    arrived = lax.all_to_all(blocks, axis, split_axis=0, concat_axis=0, tiled=True)
    return arrived.sum(axis=0)


def direction(index, length):
    return ((index + length // 2) % length - length // 2).astype(jnp.float32) * (0.5 / length)


def angle_table(first, second, length):
    product = (
        jnp.arange(first, dtype=jnp.int32)[:, None]
        * jnp.arange(second, dtype=jnp.int32)[None, :]
        % length
    )
    angles = product.astype(jnp.float32) * (2.0 * math.pi / length)
    return (jnp.cos(angles), jnp.sin(angles))


def split_length(length):
    inner_len = math.gcd(length, 128)
    return (length // inner_len, inner_len)


def transform_last(real_part, imag_part):
    length = real_part.shape[-1]
    outer_len, inner_len = split_length(length)
    real_grid = real_part.reshape(-1, outer_len, inner_len)
    imag_grid = imag_part.reshape(-1, outer_len, inner_len)
    cos_one, sin_one = angle_table(outer_len, outer_len, outer_len)
    first_re = jnp.einsum("rab,ak->rkb", real_grid, cos_one, precision=HIGHEST) - jnp.einsum(
        "rab,ak->rkb", imag_grid, sin_one, precision=HIGHEST
    )
    first_im = jnp.einsum("rab,ak->rkb", real_grid, sin_one, precision=HIGHEST) + jnp.einsum(
        "rab,ak->rkb", imag_grid, cos_one, precision=HIGHEST
    )
    cos_tw, sin_tw = angle_table(outer_len, inner_len, length)
    twist_re = first_re * cos_tw - first_im * sin_tw
    twist_im = first_re * sin_tw + first_im * cos_tw
    cos_two, sin_two = angle_table(inner_len, inner_len, inner_len)
    out_re = jnp.einsum("rkb,bq->rqk", twist_re, cos_two, precision=HIGHEST) - jnp.einsum(
        "rkb,bq->rqk", twist_im, sin_two, precision=HIGHEST
    )
    out_im = jnp.einsum("rkb,bq->rqk", twist_re, sin_two, precision=HIGHEST) + jnp.einsum(
        "rkb,bq->rqk", twist_im, cos_two, precision=HIGHEST
    )
    return (out_re.reshape(-1, length), out_im.reshape(-1, length))


def transform_first(real_part, imag_part):
    length = real_part.shape[0]
    outer_len, inner_len = split_length(length)
    real_grid = real_part.reshape(outer_len, inner_len, -1)
    imag_grid = imag_part.reshape(outer_len, inner_len, -1)
    cos_one, sin_one = angle_table(outer_len, outer_len, outer_len)
    first_re = jnp.einsum("abc,ak->kbc", real_grid, cos_one, precision=HIGHEST) - jnp.einsum(
        "abc,ak->kbc", imag_grid, sin_one, precision=HIGHEST
    )
    first_im = jnp.einsum("abc,ak->kbc", real_grid, sin_one, precision=HIGHEST) + jnp.einsum(
        "abc,ak->kbc", imag_grid, cos_one, precision=HIGHEST
    )
    cos_tw, sin_tw = angle_table(outer_len, inner_len, length)
    twist_re = first_re * cos_tw[:, :, None] - first_im * sin_tw[:, :, None]
    twist_im = first_re * sin_tw[:, :, None] + first_im * cos_tw[:, :, None]
    cos_two, sin_two = angle_table(inner_len, inner_len, inner_len)
    out_re = jnp.einsum("kbc,bq->qkc", twist_re, cos_two, precision=HIGHEST) - jnp.einsum(
        "kbc,bq->qkc", twist_im, sin_two, precision=HIGHEST
    )
    out_im = jnp.einsum("kbc,bq->qkc", twist_re, sin_two, precision=HIGHEST) + jnp.einsum(
        "kbc,bq->qkc", twist_im, cos_two, precision=HIGHEST
    )
    return (out_re.reshape(length, -1), out_im.reshape(length, -1))


def grid_block(received, taps, start, block_len, band_rows, totals):
    piece = lax.dynamic_slice_in_dim(received, start, block_len, 1)
    encoded = jnp.maximum(piece[2].astype(jnp.int32) - 1, 0)
    band_row = encoded // G
    column = encoded % G
    kernel_len = taps.shape[0]
    taps_low = taps.astype(jnp.bfloat16)
    weight_re = (taps[None, :] * piece[0][:, None]).astype(jnp.bfloat16)
    weight_im = (taps[None, :] * piece[1][:, None]).astype(jnp.bfloat16)
    rel_row = jnp.arange(band_rows, dtype=jnp.int32)[None, :] - band_row[:, None]
    rel_col = (jnp.arange(G, dtype=jnp.int32)[None, :] - column[:, None]) % G
    row_re = jnp.zeros((block_len, band_rows), jnp.bfloat16)
    row_im = jnp.zeros((block_len, band_rows), jnp.bfloat16)
    col_table = jnp.zeros((block_len, G), jnp.bfloat16)
    for tap_index in range(kernel_len):
        row_re = jnp.where(rel_row == tap_index, weight_re[:, tap_index : tap_index + 1], row_re)
        row_im = jnp.where(rel_row == tap_index, weight_im[:, tap_index : tap_index + 1], row_im)
        col_table = jnp.where(rel_col == tap_index, taps_low[tap_index], col_table)
    row_table = jnp.concatenate([row_re, row_im], axis=1)
    return totals + lax.dot_general(
        row_table, col_table, (((0,), (0,)), ((), ())), preferred_element_type=jnp.float32
    )


def local(visibility, target, offset, taps, w_plane):
    tiles = lax.axis_size(TILE)
    planes = lax.axis_size(PLANE)
    devices = tiles * planes
    vis_dev = visibility.shape[1]
    capacity = 2 * vis_dev // devices
    slot_total = devices * capacity
    band = G // tiles
    columns = G // tiles
    kernel_len = taps.shape[0]
    band_rows = band + kernel_len - 1
    destination = target[:, 0]
    onehot = (destination[:, None] == jnp.arange(devices, dtype=jnp.int32)[None, :]).astype(
        jnp.int32
    )
    rank = jnp.sum(jnp.cumsum(onehot, axis=0) * onehot, axis=1) - 1
    slot = destination * capacity + rank
    payload = jnp.stack([visibility[0], visibility[1], offset.astype(jnp.float32) + 1.0])
    outgoing = jnp.zeros((3, slot_total), jnp.float32).at[:, slot].set(payload)
    received = exchange_by_chip(
        outgoing, (("plane_0", "plane_1", "tile_0", "tile_1"), "tile_2"), (1, 0), 1, 1
    )
    block_len = min(512, slot_total)
    empty = jnp.zeros((2 * band_rows, G), jnp.float32)

    def grid_step(index, totals):
        return grid_block(received, taps, index * block_len, block_len, band_rows, totals)

    gridded = lax.fori_loop(0, slot_total // block_len, grid_step, empty)
    gridded = gridded.reshape(2, band_rows, G)
    incoming = shifted(gridded[:, band:], TILE, 1)
    grid_band = gridded[:, :band].at[:, : kernel_len - 1].add(incoming)
    col_re, col_im = transform_last(grid_band[0], grid_band[1])
    stacked = jnp.stack([col_re, col_im]).reshape(2, band, tiles, columns)
    exchanged = lax.all_to_all(stacked, TILE, split_axis=2, concat_axis=1, tiled=True)
    item_count = exchanged.shape[3]
    rows_re, rows_im = transform_first(
        exchanged[0].reshape(G, item_count), exchanged[1].reshape(G, item_count)
    )
    image_parts = jnp.stack([rows_re, rows_im]).reshape(2, G, 1, item_count).reshape(2, G, columns)
    line_pos = jnp.arange(G, dtype=jnp.int32)
    column_pos = lax.axis_index(TILE) * columns + jnp.arange(columns, dtype=jnp.int32)
    cos_row = direction(line_pos, G)
    cos_col = direction(column_pos, G)
    n_minus = (
        jnp.sqrt(1.0 - cos_row[:, None] * cos_row[:, None] - cos_col[None, :] * cos_col[None, :])
        - 1.0
    )
    phase = 2.0 * math.pi * w_plane[0] * n_minus
    screened = jnp.cos(phase) * image_parts[0] - jnp.sin(phase) * image_parts[1]
    summed = summed_on_arrival(screened, PLANE, 0)
    return summed * (1.0 / math.sqrt(vis_dev * devices))


def solution(mesh):
    finer = Mesh(
        mesh.devices.reshape(2, 4, 2, 4, 2), ("plane_0", "plane_1", "tile_0", "tile_1", "tile_2")
    )
    return jax.shard_map(
        local,
        mesh=finer,
        in_specs=(P(None, PLANE_TILE), P(PLANE_TILE, None), P(PLANE_TILE), P(), P(PLANE)),
        out_specs=P(PLANE, TILE),
        check_vma=False,
    )
```

profile of v0, /device:TPU:8, one launch (start us, length us, event | category | flops | bytes accessed | tf_op | source)
XLA Modules:
  0.0 555.1 jit_solution(2011988327328630223)
XLA Ops:
  2.8 6.1 %scatter_custom_fusion = f32[3,4096]{0,1:T(8,128)S(1)} fusion(s32[2048]{0:T(1024)S(1)} %bitcast.168, f32[2048,3]{1,0:T(8,128)S(1)} %copy.69, f32[]{:T(128)} %constant.337.clone.1), kind=kCustom, calls=%fused_computation.153 | custom fusion | bytes 49156 | tf_op jit(solution)/shard_map/scatter | solution.py:163
  16.3 11.7 %all-to-all-start.1 = ((f32[64,1,192]{2,1,0:T(1,128)}), f32[64,1,192]{2,1,0:T(1,128)S(1)}, u32[]{:S(2)}, u32[]{:S(2)}) async-start(f32[64,1,192]{2,1,0:T(1,128)} %reshape.301), calls=%async_computation.1 | async-start | bytes 131072 | tf_op jit(solution)/shard_map/all_to_all | solution.py:31
  28.0 8.6 %all-to-all-done.1 = f32[64,1,192]{2,1,0:T(1,128)S(1)} async-done(((f32[64,1,192]{2,1,0:T(1,128)}), f32[64,1,192]{2,1,0:T(1,128)S(1)}, u32[]{:S(2)}, u32[]{:S(2)}) %all-to-all-start.1) | async-done | bytes 49184 | tf_op jit(solution)/shard_map/all_to_all | solution.py:31
  37.8 175.1 %while.18 = (s32[]{:T(128)}, f32[526,4096]{1,0:T(8,128)}, f32[3,4096]{1,0:T(4,128)S(1)}, f32[8]{0:T(128)S(1)}, bf16[8]{0:T(256)(128)(2,1)S(1)}, /*index=5*/s32[]...) while((s32[]{:T(128)}, f32[526,4096]{1,0:T(8,128)}, f32[3,4096]{1,0:T(4,128)S(1)}, ...), condition=%wide.region_5.6_spmd.clone, body=%wide.region_4.5_spmd.clone.sunk | while | flops 2273700864 | bytes 18414876 | solution.py:173
  40.5 17.3 %select_add_fusion.2 = f32[526,4096]{1,0:T(8,128)} fusion(f32[526,4096]{1,0:T(8,128)} %get-tuple-element.356, pred[]{:T(512)S(6)} %compare.38, s32[512]{0:T(512)S(1)} %get-tuple-element.312, bf16[]{:T(256)} %bitcast.130, bf16[]{:T(256)} %bitcast.131, bf16[]{:T(256)} %bitcast.132, bf16[]{:T(256)} %bitcast.133, bf16[]{:T(256)} %bitcast.134, ...), kind=kOutput, calls=%fused_computation.4.clone.1 | convolution fusion | flops 2270310400 | bytes 17776656 | tf_op jit(solution)/shard_map/while/body/eval_jaxpr/dot_general | solution.py:140
  60.5 19.5 %select_add_fusion.2 = f32[526,4096]{1,0:T(8,128)} fusion(f32[526,4096]{1,0:T(8,128)} %get-tuple-element.356, pred[]{:T(512)S(6)} %compare.38, s32[512]{0:T(512)S(1)} %get-tuple-element.312, bf16[]{:T(256)} %bitcast.130, bf16[]{:T(256)} %bitcast.131, bf16[]{:T(256)} %bitcast.132, bf16[]{:T(256)} %bitcast.133, bf16[]{:T(256)} %bitcast.134, ...), kind=kOutput, calls=%fused_computation.4.clone.1 | convolution fusion | flops 2270310400 | bytes 17776656 | tf_op jit(solution)/shard_map/while/body/eval_jaxpr/dot_general | solution.py:140
  82.7 19.5 %select_add_fusion.2 = f32[526,4096]{1,0:T(8,128)} fusion(f32[526,4096]{1,0:T(8,128)} %get-tuple-element.356, pred[]{:T(512)S(6)} %compare.38, s32[512]{0:T(512)S(1)} %get-tuple-element.312, bf16[]{:T(256)} %bitcast.130, bf16[]{:T(256)} %bitcast.131, bf16[]{:T(256)} %bitcast.132, bf16[]{:T(256)} %bitcast.133, bf16[]{:T(256)} %bitcast.134, ...), kind=kOutput, calls=%fused_computation.4.clone.1 | convolution fusion | flops 2270310400 | bytes 17776656 | tf_op jit(solution)/shard_map/while/body/eval_jaxpr/dot_general | solution.py:140
  104.8 19.5 %select_add_fusion.2 = f32[526,4096]{1,0:T(8,128)} fusion(f32[526,4096]{1,0:T(8,128)} %get-tuple-element.356, pred[]{:T(512)S(6)} %compare.38, s32[512]{0:T(512)S(1)} %get-tuple-element.312, bf16[]{:T(256)} %bitcast.130, bf16[]{:T(256)} %bitcast.131, bf16[]{:T(256)} %bitcast.132, bf16[]{:T(256)} %bitcast.133, bf16[]{:T(256)} %bitcast.134, ...), kind=kOutput, calls=%fused_computation.4.clone.1 | convolution fusion | flops 2270310400 | bytes 17776656 | tf_op jit(solution)/shard_map/while/body/eval_jaxpr/dot_general | solution.py:140
  127.0 19.5 %select_add_fusion.2 = f32[526,4096]{1,0:T(8,128)} fusion(f32[526,4096]{1,0:T(8,128)} %get-tuple-element.356, pred[]{:T(512)S(6)} %compare.38, s32[512]{0:T(512)S(1)} %get-tuple-element.312, bf16[]{:T(256)} %bitcast.130, bf16[]{:T(256)} %bitcast.131, bf16[]{:T(256)} %bitcast.132, bf16[]{:T(256)} %bitcast.133, bf16[]{:T(256)} %bitcast.134, ...), kind=kOutput, calls=%fused_computation.4.clone.1 | convolution fusion | flops 2270310400 | bytes 17776656 | tf_op jit(solution)/shard_map/while/body/eval_jaxpr/dot_general | solution.py:140
  149.1 19.5 %select_add_fusion.2 = f32[526,4096]{1,0:T(8,128)} fusion(f32[526,4096]{1,0:T(8,128)} %get-tuple-element.356, pred[]{:T(512)S(6)} %compare.38, s32[512]{0:T(512)S(1)} %get-tuple-element.312, bf16[]{:T(256)} %bitcast.130, bf16[]{:T(256)} %bitcast.131, bf16[]{:T(256)} %bitcast.132, bf16[]{:T(256)} %bitcast.133, bf16[]{:T(256)} %bitcast.134, ...), kind=kOutput, calls=%fused_computation.4.clone.1 | convolution fusion | flops 2270310400 | bytes 17776656 | tf_op jit(solution)/shard_map/while/body/eval_jaxpr/dot_general | solution.py:140
  171.3 19.5 %select_add_fusion.2 = f32[526,4096]{1,0:T(8,128)} fusion(f32[526,4096]{1,0:T(8,128)} %get-tuple-element.356, pred[]{:T(512)S(6)} %compare.38, s32[512]{0:T(512)S(1)} %get-tuple-element.312, bf16[]{:T(256)} %bitcast.130, bf16[]{:T(256)} %bitcast.131, bf16[]{:T(256)} %bitcast.132, bf16[]{:T(256)} %bitcast.133, bf16[]{:T(256)} %bitcast.134, ...), kind=kOutput, calls=%fused_computation.4.clone.1 | convolution fusion | flops 2270310400 | bytes 17776656 | tf_op jit(solution)/shard_map/while/body/eval_jaxpr/dot_general | solution.py:140
  193.5 19.5 %select_add_fusion.2 = f32[526,4096]{1,0:T(8,128)} fusion(f32[526,4096]{1,0:T(8,128)} %get-tuple-element.356, pred[]{:T(512)S(6)} %compare.38, s32[512]{0:T(512)S(1)} %get-tuple-element.312, bf16[]{:T(256)} %bitcast.130, bf16[]{:T(256)} %bitcast.131, bf16[]{:T(256)} %bitcast.132, bf16[]{:T(256)} %bitcast.133, bf16[]{:T(256)} %bitcast.134, ...), kind=kOutput, calls=%fused_computation.4.clone.1 | convolution fusion | flops 2270310400 | bytes 17776656 | tf_op jit(solution)/shard_map/while/body/eval_jaxpr/dot_general | solution.py:140
  213.0 7.6 %reshape.264 = f32[2,263,4096]{2,1,0:T(8,128)} reshape(f32[526,4096]{1,0:T(8,128)} %get-tuple-element.158) | data formatting | bytes 17235968 | tf_op jit(solution)/shard_map/reshape | solution.py:174
  221.7 7.6 %slice.405 = f32[2,256,4096]{2,1,0:T(8,128)} slice(f32[2,263,4096]{2,1,0:T(8,128)} %reshape.264), slice={[0:2], [0:256], [0:4096]} | slice | bytes 16777216 | tf_op jit(solution)/shard_map/slice | solution.py:176
  250.3 5.1 subtract_bitcast_fusion.1
  255.4 6.2 %fusion.84 = f32[128,256,32]{1,0,2:T(8,128)S(1)} fusion(f32[256,32,128]{2,1,0:T(8,128)S(1)} %get-tuple-element.234), kind=kOutput, calls=%fused_computation.135 | convolution fusion | flops 1610842112 | bytes 8388608 | tf_op jit(solution)/shard_map/rkb,bq->rqk/dot_general | solution.py:87
  261.7 6.2 %fusion.82 = f32[128,256,32]{1,0,2:T(8,128)S(1)} fusion(f32[256,32,128]{2,1,0:T(8,128)S(1)} %get-tuple-element.234), kind=kOutput, calls=%fused_computation.133 | convolution fusion | flops 1610842112 | bytes 8388608 | tf_op jit(solution)/shard_map/rkb,bq->rqk/dot_general | solution.py:90
  267.9 6.8 %subtract_bitcast_fusion = f32[256,128,32]{0,1,2:T(8,128)S(1)} fusion(f32[128,256,32]{1,0,2:T(8,128)S(1)} %fusion.84, f32[256,32,128]{2,1,0:T(8,128)S(1)} %get-tuple-element.233), kind=kOutput, calls=%fused_computation.114 | convolution fusion | flops 1611890688 | bytes 12582912 | tf_op jit(solution)/shard_map/rkb,bq->rqk/dot_general | solution.py:87
  277.1 6.1 %add_bitcast_fusion = f32[256,128,32]{0,1,2:T(8,128)S(1)} fusion(f32[128,256,32]{1,0,2:T(8,128)S(1)} %fusion.82, f32[256,32,128]{2,1,0:T(8,128)S(1)} %get-tuple-element.233), kind=kOutput, calls=%fused_computation.113 | convolution fusion | flops 1611890688 | bytes 12582912 | tf_op jit(solution)/shard_map/rkb,bq->rqk/dot_general | solution.py:90
  290.5 6.6 %all-to-all-start.2 = ((f32[2,256,16,256]{1,3,0,2:T(8,128)}), f32[2,256,16,256]{1,3,0,2:T(8,128)}, u32[]{:S(2)}, u32[]{:S(2)}) async-start(f32[2,256,16,256]{1,3,0,2:T(8,128)} %copy.80), calls=%async_computation.2 | async-start | bytes 16777216 | tf_op jit(solution)/shard_map/all_to_all | solution.py:179
  298.0 112.6 %all-to-all-done.2 = f32[2,256,16,256]{1,3,0,2:T(8,128)} async-done(((f32[2,256,16,256]{1,3,0,2:T(8,128)}), f32[2,256,16,256]{1,3,0,2:T(8,128)}, u32[]{:S(2)}, u32[]{:S(2)}) %all-to-all-start.2) | async-done | bytes 8388640 | tf_op jit(solution)/shard_map/all_to_all | solution.py:179
  410.6 8.7 %copy.81 = f32[2,256,16,256]{3,1,2,0:T(8,128)} copy(f32[2,256,16,256]{1,3,0,2:T(8,128)} %all-to-all-done.2) | data formatting | bytes 16777216 | tf_op jit(solution)/shard_map/all_to_all | solution.py:179
  423.3 5.9 %fusion.76 = f32[32,128,256]{2,0,1:T(8,128)S(1)} fusion(f32[32,128,256]{2,1,0:T(8,128)S(1)} %bitcast.146), kind=kOutput, calls=%fused_computation.127 | convolution fusion | flops 402667520 | bytes 8388608 | tf_op jit(solution)/shard_map/abc,ak->kbc/dot_general | solution.py:102
  429.2 6.6 %fusion.74 = f32[32,128,256]{2,0,1:T(8,128)S(1)} fusion(f32[32,128,256]{2,1,0:T(8,128)S(1)} %bitcast.147), kind=kOutput, calls=%fused_computation.125 | convolution fusion | flops 402667520 | bytes 8388608 | tf_op jit(solution)/shard_map/abc,ak->kbc/dot_general | solution.py:105
  435.8 6.2 %fusion.94 = f32[32,128,256]{2,0,1:T(8,128)S(1)} fusion(f32[32,128,256]{2,0,1:T(8,128)S(1)} %fusion.76, f32[32,128,256]{2,1,0:T(8,128)S(1)} %bitcast.142), kind=kOutput, calls=%fused_computation.141 | convolution fusion | flops 403716096 | bytes 12582912 | tf_op jit(solution)/shard_map/abc,ak->kbc/dot_general | solution.py:102
  441.9 7.9 %multiply_subtract_fusion = (f32[32,128,256]{2,0,1:T(8,128)S(1)}, f32[32,128,256]{2,0,1:T(8,128)S(1)}) fusion(f32[32,128,256]{2,0,1:T(8,128)S(1)} %fusion.94, f32[32,128]{0,1:T(8,128)S(1)} %copy.87, f32[32,128]{0,1:T(8,128)S(1)} %copy.84, f32[32,128,256]{2,0,1:T(8,128)S(1)} %fusion.74, f32[32,128,256]{2,1,0:T(8,128)S(1)} %bitcast.143), kind=kOutput, calls=%fused_computation.112 | convolution fusion | flops 410007552 | bytes 21004288 | tf_op jit(solution)/shard_map/abc,ak->kbc/dot_general | solution.py:105
  449.9 6.0 %fusion.68 = f32[128,32,256]{2,0,1:T(8,128)S(1)} fusion(f32[32,128,256]{2,0,1:T(8,128)S(1)} %get-tuple-element.232), kind=kOutput, calls=%fused_computation.119 | convolution fusion | flops 1610842112 | bytes 8388608 | tf_op jit(solution)/shard_map/kbc,bq->qkc/dot_general | solution.py:112
  455.9 6.5 %fusion.66 = f32[128,32,256]{2,0,1:T(8,128)S(1)} fusion(f32[32,128,256]{2,0,1:T(8,128)S(1)} %get-tuple-element.232), kind=kOutput, calls=%fused_computation.117 | convolution fusion | flops 1610842112 | bytes 8388608 | tf_op jit(solution)/shard_map/kbc,bq->qkc/dot_general | solution.py:115
  462.4 6.0 %fusion.100 = f32[128,32,256]{2,0,1:T(8,128)S(1)} fusion(f32[128,32,256]{2,0,1:T(8,128)S(1)} %fusion.68, f32[32,128,256]{2,0,1:T(8,128)S(1)} %get-tuple-element.231), kind=kOutput, calls=%fused_computation.143 | convolution fusion | flops 1611890688 | bytes 12582912 | tf_op jit(solution)/shard_map/kbc,bq->qkc/dot_general | solution.py:112
  470.8 6.5 %fusion.103 = f32[128,32,256]{2,0,1:T(8,128)S(1)} fusion(f32[128,32,256]{2,0,1:T(8,128)S(1)} %fusion.66, f32[32,128,256]{2,0,1:T(8,128)S(1)} %get-tuple-element.231), kind=kOutput, calls=%fused_computation.144 | convolution fusion | flops 1611890688 | bytes 12582912 | tf_op jit(solution)/shard_map/kbc,bq->qkc/dot_general | solution.py:115
  479.8 16.9 %fusion.65 = f32[8,512,256]{2,1,0:T(8,128)S(1)} fusion(f32[256]{0:T(256)S(1)} %fusion.179, f32[8,512]{1,0:T(8,128)S(1)} %fusion.141, f32[]{:T(128)} %bitcast, f32[8,512,256]{2,1,0:T(8,128)S(1)} %bitcast.150, f32[8,512,256]{2,1,0:T(8,128)S(1)} %bitcast.149), kind=kLoop, calls=%fused_computation.109 | loop fusion | flops 6291456 | bytes 12600324 | tf_op jit(solution)/shard_map/sub | solution.py:194
  496.8 54.5 %all_to_all.31 = f32[8,512,256]{2,1,0:T(8,128)} all-to-all(f32[8,512,256]{2,1,0:T(8,128)S(1)} %fusion.65), channel_id=1, replica_groups=mesh['plane_0'=2,'plane_1'=4,'tile_0'=2,'tile_1'=4,'tile_2'=2] {'plane_0..., dimensions={0} | all-to-all | bytes 8388608 | tf_op jit(solution)/shard_map/all_to_all | solution.py:48
  (125 shorter events, 76.4 us)
Async XLA Ops:
  0.0 1.7 copy-start
  0.0 2.4 copy-start.3
  0.0 2.4 copy-start.1
  1.7 26.3 %copy-start.2 = (f32[8]{0:T(128)S(1)}, f32[8]{0:T(128)}, u32[]{:S(2)}) copy-start(f32[8]{0:T(128)} %param.12) | copy-start | bytes 100
  16.3 20.4 %all-to-all-start.1 = ((f32[64,1,192]{2,1,0:T(1,128)}), f32[64,1,192]{2,1,0:T(1,128)S(1)}, u32[]{:S(2)}, u32[]{:S(2)}) async-start(f32[64,1,192]{2,1,0:T(1,128)} %reshape.301), calls=%async_computation.1 | async-start | bytes 131072 | tf_op jit(solution)/shard_map/all_to_all | solution.py:31
  221.5 7.8 %collective-permute-start = (f32[2,7,4096]{2,1,0:T(8,128)S(1)}, f32[2,7,4096]{2,1,0:T(8,128)S(1)}, u32[]{:S(2)}, u32[]{:S(2)}) collective-permute-start(f32[2,7,4096]{2,1,0:T(8,128)S(1)} %slice.407), channel_id=1, source_target_pairs={{0,1},{1,2},{2,3},{3,4},{4,5},{5,6},{6,7},{7,8},{8,9},{9,10},{10,1... | collective-permute-start | bytes 688136 | tf_op jit(solution)/shard_map/ppermute | solution.py:43
  290.5 120.1 %all-to-all-start.2 = ((f32[2,256,16,256]{1,3,0,2:T(8,128)}), f32[2,256,16,256]{1,3,0,2:T(8,128)}, u32[]{:S(2)}, u32[]{:S(2)}) async-start(f32[2,256,16,256]{1,3,0,2:T(8,128)} %copy.80), calls=%async_computation.2 | async-start | bytes 16777216 | tf_op jit(solution)/shard_map/all_to_all | solution.py:179
where the time goes:
time: 561 us; the launch traced here: 555 us
  matrix products  248 us (44%)
  waiting for transfers between devices  121 us (22%)
  local copies, waits for them, and re-layouts  67.9 us (12%)
  blocking collectives  58.3 us (10%)
  other arithmetic  39.3 us (7%)
  starting transfers between devices  18.4 us (3%)
    dot_general x8, matrix products, grid_block(): lax.dot_general(row_table, col_table, (((0,), (0,)), ((), ())), preferred...  154 us
    all_to_all x1, waiting for transfers between devices, local(): lax.all_to_all(stacked, TILE, split_axis=2, concat_axis=1, tiled=True)  113 us
    all_to_all x1, blocking collectives, summed_on_arrival(): lax.all_to_all(blocks, axis, split_axis=0, concat_axis=0, tiled=True)  54.5 us
    sub x1, other arithmetic, local(): screened = jnp.cos(phase) * image_parts[0] - jnp.sin(phase) * image_parts[1]  16.9 us
    select_n x8, other arithmetic, grid_block(): jnp.where(rel_row == tap_index, weight_re[:, tap_index:tap_index + 1], ro...  12.7 us
    all_to_all x1, starting transfers between devices, moved_by_axis(): lax.all_to_all(blocks, axes[k], split_axis=k, concat_axis=k, tiled=True)  11.7 us
  transfers between devices with their start and end apart: 3, of which 2 were waited for; matrix products, arithmetic and copies ran while one was open for 1% of the time, Pallas kernels for 0%

commit v1 on v0

--- a/solution.py
+++ b/solution.py
@@ -176,7 +176,9 @@
     grid_band = gridded[:, :band].at[:, : kernel_len - 1].add(incoming)
     col_re, col_im = transform_last(grid_band[0], grid_band[1])
     stacked = jnp.stack([col_re, col_im]).reshape(2, band, tiles, columns)
-    exchanged = lax.all_to_all(stacked, TILE, split_axis=2, concat_axis=1, tiled=True)
+    shards = jnp.split(stacked, lax.axis_size(TILE), axis=2)
+    arrived_2 = lax.all_to_all(jnp.stack(shards), TILE, 0, 0)
+    exchanged = jnp.concatenate(arrived_2, axis=1)
     item_count = exchanged.shape[3]
     rows_re, rows_im = transform_first(
         exchanged[0].reshape(G, item_count), exchanged[1].reshape(G, item_count)

time: 561 us -> 584 us (1.041)
  other arithmetic: 39.3 us -> 52.1 us
  matrix products: 248 us -> 257 us
    unnamed x1 -> x16, other arithmetic: 0.01 us -> 12.9 us
    slice x1 -> x2, local copies, waits for them, and re-layouts: 4.01 us -> 13.3 us  [local(): exchanged[0].reshape(G, item_count)]
    all_to_all x1 -> x0, local copies, waits for them, and re-layouts: 8.69 us -> none  [local(): lax.all_to_all(stacked, TILE, split_axis=2, concat_axis=1, tiled=True)]
where the time goes in v1:
time: 584 us; the launch traced here: 579 us
  matrix products  257 us (44%)
  waiting for transfers between devices  121 us (21%)
  local copies, waits for them, and re-layouts  69.9 us (12%)
  blocking collectives  58.3 us (10%)
  other arithmetic  52.1 us (9%)
  starting transfers between devices  18.7 us (3%)
    dot_general x8, matrix products, grid_block(): lax.dot_general(row_table, col_table, (((0,), (0,)), ((), ())), preferred...  154 us
    all_to_all x1, waiting for transfers between devices, local(): arrived_2 = lax.all_to_all(jnp.stack(shards), TILE, 0, 0)  113 us
    all_to_all x1, blocking collectives, summed_on_arrival(): lax.all_to_all(blocks, axis, split_axis=0, concat_axis=0, tiled=True)  54.5 us
    sub x1, other arithmetic, local(): screened = jnp.cos(phase) * image_parts[0] - jnp.sin(phase) * image_parts[1]  16.9 us
    slice x2, local copies, waits for them, and re-layouts, local(): exchanged[0].reshape(G, item_count)  13.3 us
    unnamed x16, other arithmetic  12.9 us
    select_n x8, other arithmetic, grid_block(): jnp.where(rel_row == tap_index, weight_re[:, tap_index:tap_index + 1], ro...  12.7 us
    all_to_all x1, starting transfers between devices, moved_by_axis(): lax.all_to_all(blocks, axes[k], split_axis=k, concat_axis=k, tiled=True)  12 us
  transfers between devices with their start and end apart: 3, of which 2 were waited for; matrix products, arithmetic and copies ran while one was open for 1% of the time, Pallas kernels for 0%

profile of v1, /device:TPU:8, one launch (start us, length us, event | category | flops | bytes accessed | tf_op | source)
XLA Modules:
  0.0 578.8 jit_solution(16028138509123439256)
XLA Ops:
  2.8 6.1 %scatter_custom_fusion = f32[3,4096]{0,1:T(8,128)S(1)} fusion(s32[2048]{0:T(1024)S(1)} %bitcast.259, f32[2048,3]{1,0:T(8,128)S(1)} %copy.99, f32[]{:T(128)} %constant.337.clone.1), kind=kCustom, calls=%fused_computation.182 | custom fusion | bytes 49156 | tf_op jit(solution)/shard_map/scatter | solution.py:163
  16.3 12.0 %all-to-all-start.1 = ((f32[64,1,192]{2,1,0:T(1,128)}), f32[64,1,192]{2,1,0:T(1,128)S(1)}, u32[]{:S(2)}, u32[]{:S(2)}) async-start(f32[64,1,192]{2,1,0:T(1,128)} %reshape.306), calls=%async_computation.1 | async-start | bytes 131072 | tf_op jit(solution)/shard_map/all_to_all | solution.py:31
  28.4 8.6 %all-to-all-done.1 = f32[64,1,192]{2,1,0:T(1,128)S(1)} async-done(((f32[64,1,192]{2,1,0:T(1,128)}), f32[64,1,192]{2,1,0:T(1,128)S(1)}, u32[]{:S(2)}, u32[]{:S(2)}) %all-to-all-start.1) | async-done | bytes 49184 | tf_op jit(solution)/shard_map/all_to_all | solution.py:31
  38.1 175.1 %while.18 = (s32[]{:T(128)}, f32[526,4096]{1,0:T(8,128)}, f32[3,4096]{1,0:T(4,128)S(1)}, f32[8]{0:T(128)S(1)}, bf16[8]{0:T(256)(128)(2,1)S(1)}, /*index=5*/s32[]...) while((s32[]{:T(128)}, f32[526,4096]{1,0:T(8,128)}, f32[3,4096]{1,0:T(4,128)S(1)}, ...), condition=%wide.region_5.6_spmd.clone, body=%wide.region_4.5_spmd.clone.sunk | while | flops 2273700864 | bytes 18414876 | solution.py:173
  40.8 17.3 %select_add_fusion.2 = f32[526,4096]{1,0:T(8,128)} fusion(f32[526,4096]{1,0:T(8,128)} %get-tuple-element.356, pred[]{:T(512)S(6)} %compare.38, s32[512]{0:T(512)S(1)} %get-tuple-element.312, bf16[]{:T(256)} %bitcast.192, bf16[]{:T(256)} %bitcast.193, bf16[]{:T(256)} %bitcast.194, bf16[]{:T(256)} %bitcast.195, bf16[]{:T(256)} %bitcast.196, ...), kind=kOutput, calls=%fused_computation.4.clone.1 | convolution fusion | flops 2270310400 | bytes 17776656 | tf_op jit(solution)/shard_map/while/body/eval_jaxpr/dot_general | solution.py:140
  60.8 19.5 %select_add_fusion.2 = f32[526,4096]{1,0:T(8,128)} fusion(f32[526,4096]{1,0:T(8,128)} %get-tuple-element.356, pred[]{:T(512)S(6)} %compare.38, s32[512]{0:T(512)S(1)} %get-tuple-element.312, bf16[]{:T(256)} %bitcast.192, bf16[]{:T(256)} %bitcast.193, bf16[]{:T(256)} %bitcast.194, bf16[]{:T(256)} %bitcast.195, bf16[]{:T(256)} %bitcast.196, ...), kind=kOutput, calls=%fused_computation.4.clone.1 | convolution fusion | flops 2270310400 | bytes 17776656 | tf_op jit(solution)/shard_map/while/body/eval_jaxpr/dot_general | solution.py:140
  83.0 19.5 %select_add_fusion.2 = f32[526,4096]{1,0:T(8,128)} fusion(f32[526,4096]{1,0:T(8,128)} %get-tuple-element.356, pred[]{:T(512)S(6)} %compare.38, s32[512]{0:T(512)S(1)} %get-tuple-element.312, bf16[]{:T(256)} %bitcast.192, bf16[]{:T(256)} %bitcast.193, bf16[]{:T(256)} %bitcast.194, bf16[]{:T(256)} %bitcast.195, bf16[]{:T(256)} %bitcast.196, ...), kind=kOutput, calls=%fused_computation.4.clone.1 | convolution fusion | flops 2270310400 | bytes 17776656 | tf_op jit(solution)/shard_map/while/body/eval_jaxpr/dot_general | solution.py:140
  105.1 19.5 %select_add_fusion.2 = f32[526,4096]{1,0:T(8,128)} fusion(f32[526,4096]{1,0:T(8,128)} %get-tuple-element.356, pred[]{:T(512)S(6)} %compare.38, s32[512]{0:T(512)S(1)} %get-tuple-element.312, bf16[]{:T(256)} %bitcast.192, bf16[]{:T(256)} %bitcast.193, bf16[]{:T(256)} %bitcast.194, bf16[]{:T(256)} %bitcast.195, bf16[]{:T(256)} %bitcast.196, ...), kind=kOutput, calls=%fused_computation.4.clone.1 | convolution fusion | flops 2270310400 | bytes 17776656 | tf_op jit(solution)/shard_map/while/body/eval_jaxpr/dot_general | solution.py:140
  127.3 19.5 %select_add_fusion.2 = f32[526,4096]{1,0:T(8,128)} fusion(f32[526,4096]{1,0:T(8,128)} %get-tuple-element.356, pred[]{:T(512)S(6)} %compare.38, s32[512]{0:T(512)S(1)} %get-tuple-element.312, bf16[]{:T(256)} %bitcast.192, bf16[]{:T(256)} %bitcast.193, bf16[]{:T(256)} %bitcast.194, bf16[]{:T(256)} %bitcast.195, bf16[]{:T(256)} %bitcast.196, ...), kind=kOutput, calls=%fused_computation.4.clone.1 | convolution fusion | flops 2270310400 | bytes 17776656 | tf_op jit(solution)/shard_map/while/body/eval_jaxpr/dot_general | solution.py:140
  149.5 19.5 %select_add_fusion.2 = f32[526,4096]{1,0:T(8,128)} fusion(f32[526,4096]{1,0:T(8,128)} %get-tuple-element.356, pred[]{:T(512)S(6)} %compare.38, s32[512]{0:T(512)S(1)} %get-tuple-element.312, bf16[]{:T(256)} %bitcast.192, bf16[]{:T(256)} %bitcast.193, bf16[]{:T(256)} %bitcast.194, bf16[]{:T(256)} %bitcast.195, bf16[]{:T(256)} %bitcast.196, ...), kind=kOutput, calls=%fused_computation.4.clone.1 | convolution fusion | flops 2270310400 | bytes 17776656 | tf_op jit(solution)/shard_map/while/body/eval_jaxpr/dot_general | solution.py:140
  171.6 19.5 %select_add_fusion.2 = f32[526,4096]{1,0:T(8,128)} fusion(f32[526,4096]{1,0:T(8,128)} %get-tuple-element.356, pred[]{:T(512)S(6)} %compare.38, s32[512]{0:T(512)S(1)} %get-tuple-element.312, bf16[]{:T(256)} %bitcast.192, bf16[]{:T(256)} %bitcast.193, bf16[]{:T(256)} %bitcast.194, bf16[]{:T(256)} %bitcast.195, bf16[]{:T(256)} %bitcast.196, ...), kind=kOutput, calls=%fused_computation.4.clone.1 | convolution fusion | flops 2270310400 | bytes 17776656 | tf_op jit(solution)/shard_map/while/body/eval_jaxpr/dot_general | solution.py:140
  193.8 19.5 %select_add_fusion.2 = f32[526,4096]{1,0:T(8,128)} fusion(f32[526,4096]{1,0:T(8,128)} %get-tuple-element.356, pred[]{:T(512)S(6)} %compare.38, s32[512]{0:T(512)S(1)} %get-tuple-element.312, bf16[]{:T(256)} %bitcast.192, bf16[]{:T(256)} %bitcast.193, bf16[]{:T(256)} %bitcast.194, bf16[]{:T(256)} %bitcast.195, bf16[]{:T(256)} %bitcast.196, ...), kind=kOutput, calls=%fused_computation.4.clone.1 | convolution fusion | flops 2270310400 | bytes 17776656 | tf_op jit(solution)/shard_map/while/body/eval_jaxpr/dot_general | solution.py:140
  213.3 7.6 %reshape.268 = f32[2,263,4096]{2,1,0:T(8,128)} reshape(f32[526,4096]{1,0:T(8,128)} %get-tuple-element.158) | data formatting | bytes 17235968 | tf_op jit(solution)/shard_map/reshape | solution.py:174
  222.0 7.6 %slice.405 = f32[2,256,4096]{2,1,0:T(8,128)} slice(f32[2,263,4096]{2,1,0:T(8,128)} %reshape.268), slice={[0:2], [0:256], [0:4096]} | slice | bytes 16777216 | tf_op jit(solution)/shard_map/slice | solution.py:176
  255.5 6.4 %fusion.84 = f32[128,256,32]{1,0,2:T(8,128)S(1)} fusion(f32[256,32,128]{2,1,0:T(8,128)S(1)} %get-tuple-element.234), kind=kOutput, calls=%fused_computation.164 | convolution fusion | flops 1610842112 | bytes 8388608 | tf_op jit(solution)/shard_map/rkb,bq->rqk/dot_general | solution.py:87
  262.0 6.2 %fusion.82 = f32[128,256,32]{1,0,2:T(8,128)S(1)} fusion(f32[256,32,128]{2,1,0:T(8,128)S(1)} %get-tuple-element.234), kind=kOutput, calls=%fused_computation.162 | convolution fusion | flops 1610842112 | bytes 8388608 | tf_op jit(solution)/shard_map/rkb,bq->rqk/dot_general | solution.py:90
  268.2 6.5 %subtract_bitcast_fusion = f32[256,128,32]{0,1,2:T(8,128)S(1)} fusion(f32[128,256,32]{1,0,2:T(8,128)S(1)} %fusion.84, f32[256,32,128]{2,1,0:T(8,128)S(1)} %get-tuple-element.233), kind=kOutput, calls=%fused_computation.143 | convolution fusion | flops 1611890688 | bytes 12582912 | tf_op jit(solution)/shard_map/rkb,bq->rqk/dot_general | solution.py:87
  277.1 6.2 %add_bitcast_fusion = f32[256,128,32]{0,1,2:T(8,128)S(1)} fusion(f32[128,256,32]{1,0,2:T(8,128)S(1)} %fusion.82, f32[256,32,128]{2,1,0:T(8,128)S(1)} %get-tuple-element.233), kind=kOutput, calls=%fused_computation.142 | convolution fusion | flops 1611890688 | bytes 12582912 | tf_op jit(solution)/shard_map/rkb,bq->rqk/dot_general | solution.py:90
  299.6 6.6 %all-to-all-start.2 = ((f32[16,2,256,1,256]{2,4,1,3,0:T(8,128)}), f32[16,2,256,1,256]{2,4,1,3,0:T(8,128)}, u32[]{:S(2)}, u32[]{:S(2)}) async-start(f32[16,2,256,1,256]{2,4,1,3,0:T(8,128)} %fusion.127), calls=%async_computation.2 | async-start | bytes 16777216 | tf_op jit(solution)/shard_map/all_to_all | solution.py:180
  307.0 112.6 %all-to-all-done.2 = f32[16,2,256,1,256]{2,4,1,3,0:T(8,128)} async-done(((f32[16,2,256,1,256]{2,4,1,3,0:T(8,128)}), f32[16,2,256,1,256]{2,4,1,3,0:T(8,128)}, u32[]{:S(2)}, u32[]{:S(2)}) %all-to-all-start.2) | async-done | bytes 8388640 | tf_op jit(solution)/shard_map/all_to_all | solution.py:180
  419.6 7.6 %fusion.264 = (f32[1,16,256,1,256]{2,4,0,3,1:T(8,128)}, f32[1,16,256,1,256]{2,4,0,3,1:T(8,128)}) fusion(f32[2,16,256,1,256]{2,4,0,3,1:T(8,128)} %bitcast.41), kind=kLoop, calls=%fused_computation.359 | loop fusion | bytes 16777216 | tf_op jit(solution)/shard_map/slice | solution.py:184
  432.5 10.1 %fusion.76 = f32[32,128,256]{2,0,1:T(8,128)} fusion(f32[32,128,256]{2,1,0:T(8,128)} %bitcast.240), kind=kOutput, calls=%fused_computation.156 | convolution fusion | flops 402667520 | bytes 8388608 | tf_op jit(solution)/shard_map/abc,ak->kbc/dot_general | solution.py:102
  442.7 7.0 %fusion.74 = f32[32,128,256]{2,0,1:T(8,128)} fusion(f32[32,128,256]{2,1,0:T(8,128)S(1)} %bitcast.241), kind=kOutput, calls=%fused_computation.154 | convolution fusion | flops 402667520 | bytes 8388608 | tf_op jit(solution)/shard_map/abc,ak->kbc/dot_general | solution.py:105
  449.6 5.7 copy.125
  455.4 10.0 %fusion.94 = f32[32,128,256]{2,0,1:T(8,128)S(1)} fusion(f32[32,128,256]{2,0,1:T(8,128)} %fusion.76, f32[32,128,256]{2,1,0:T(8,128)} %bitcast.234), kind=kOutput, calls=%fused_computation.170 | convolution fusion | flops 403716096 | bytes 12582912 | tf_op jit(solution)/shard_map/abc,ak->kbc/dot_general | solution.py:102
  465.4 7.8 %multiply_subtract_fusion = (f32[32,128,256]{2,0,1:T(8,128)S(1)}, f32[32,128,256]{2,0,1:T(8,128)S(1)}) fusion(f32[32,128,256]{2,0,1:T(8,128)S(1)} %fusion.94, f32[32,128]{0,1:T(8,128)S(1)} %copy.132, f32[32,128]{0,1:T(8,128)S(1)} %copy.129, f32[32,128,256]{2,0,1:T(8,128)S(1)} %copy-done.2, f32[32,128,256]{2,1,0:T(8,128)S(1)} %bitcast.235), kind=kOutput, calls=%fused_computation.141 | convolution fusion | flops 410007552 | bytes 21004288 | tf_op jit(solution)/shard_map/abc,ak->kbc/dot_general | solution.py:105
  473.3 6.0 %fusion.68 = f32[128,32,256]{2,0,1:T(8,128)S(1)} fusion(f32[32,128,256]{2,0,1:T(8,128)S(1)} %get-tuple-element.232), kind=kOutput, calls=%fused_computation.148 | convolution fusion | flops 1610842112 | bytes 8388608 | tf_op jit(solution)/shard_map/kbc,bq->qkc/dot_general | solution.py:112
  479.3 6.2 %fusion.66 = f32[128,32,256]{2,0,1:T(8,128)S(1)} fusion(f32[32,128,256]{2,0,1:T(8,128)S(1)} %get-tuple-element.232), kind=kOutput, calls=%fused_computation.146 | convolution fusion | flops 1610842112 | bytes 8388608 | tf_op jit(solution)/shard_map/kbc,bq->qkc/dot_general | solution.py:115
  485.5 6.4 %fusion.100 = f32[128,32,256]{2,0,1:T(8,128)S(1)} fusion(f32[128,32,256]{2,0,1:T(8,128)S(1)} %fusion.68, f32[32,128,256]{2,0,1:T(8,128)S(1)} %get-tuple-element.231), kind=kOutput, calls=%fused_computation.172 | convolution fusion | flops 1611890688 | bytes 12582912 | tf_op jit(solution)/shard_map/kbc,bq->qkc/dot_general | solution.py:112
  494.4 6.7 %fusion.103 = f32[128,32,256]{2,0,1:T(8,128)S(1)} fusion(f32[128,32,256]{2,0,1:T(8,128)S(1)} %fusion.66, f32[32,128,256]{2,0,1:T(8,128)S(1)} %get-tuple-element.231), kind=kOutput, calls=%fused_computation.173 | convolution fusion | flops 1611890688 | bytes 12582912 | tf_op jit(solution)/shard_map/kbc,bq->qkc/dot_general | solution.py:115
  503.5 16.9 %fusion.65 = f32[8,512,256]{2,1,0:T(8,128)S(1)} fusion(f32[256]{0:T(256)S(1)} %fusion.196, f32[8,512]{1,0:T(8,128)S(1)} %fusion.158, f32[]{:T(128)} %bitcast, f32[8,512,256]{2,1,0:T(8,128)S(1)} %bitcast.243, f32[8,512,256]{2,1,0:T(8,128)S(1)} %bitcast.242), kind=kLoop, calls=%fused_computation.138 | loop fusion | flops 6291456 | bytes 12600324 | tf_op jit(solution)/shard_map/sub | solution.py:196
  520.5 54.5 %all_to_all.21 = f32[8,512,256]{2,1,0:T(8,128)} all-to-all(f32[8,512,256]{2,1,0:T(8,128)S(1)} %fusion.65), channel_id=1, replica_groups=mesh['plane_0'=2,'plane_1'=4,'tile_0'=2,'tile_1'=4,'tile_2'=2] {'plane_0..., dimensions={0} | all-to-all | bytes 8388608 | tf_op jit(solution)/shard_map/all_to_all | solution.py:48
  (146 shorter events, 91.6 us)
Async XLA Ops:
  0.0 1.7 copy-start.3
  0.0 2.4 copy-start.6
  0.0 2.4 copy-start.4
  1.7 26.6 %copy-start.5 = (f32[8]{0:T(128)S(1)}, f32[8]{0:T(128)}, u32[]{:S(2)}) copy-start(f32[8]{0:T(128)} %param.12) | copy-start | bytes 100
  16.3 20.7 %all-to-all-start.1 = ((f32[64,1,192]{2,1,0:T(1,128)}), f32[64,1,192]{2,1,0:T(1,128)S(1)}, u32[]{:S(2)}, u32[]{:S(2)}) async-start(f32[64,1,192]{2,1,0:T(1,128)} %reshape.306), calls=%async_computation.1 | async-start | bytes 131072 | tf_op jit(solution)/shard_map/all_to_all | solution.py:31
  221.9 7.8 %collective-permute-start = (f32[2,7,4096]{2,1,0:T(8,128)S(1)}, f32[2,7,4096]{2,1,0:T(8,128)S(1)}, u32[]{:S(2)}, u32[]{:S(2)}) collective-permute-start(f32[2,7,4096]{2,1,0:T(8,128)S(1)} %slice.407), channel_id=1, source_target_pairs={{0,1},{1,2},{2,3},{3,4},{4,5},{5,6},{6,7},{7,8},{8,9},{9,10},{10,1... | collective-permute-start | bytes 688136 | tf_op jit(solution)/shard_map/ppermute | solution.py:43
  299.6 120.1 %all-to-all-start.2 = ((f32[16,2,256,1,256]{2,4,1,3,0:T(8,128)}), f32[16,2,256,1,256]{2,4,1,3,0:T(8,128)}, u32[]{:S(2)}, u32[]{:S(2)}) async-start(f32[16,2,256,1,256]{2,4,1,3,0:T(8,128)} %fusion.127), calls=%async_computation.2 | async-start | bytes 16777216 | tf_op jit(solution)/shard_map/all_to_all | solution.py:180
  432.5 10.1 %copy-start.1 = (f32[1,16,256,1,256]{4,2,1,3,0:T(8,128)S(1)}, f32[1,16,256,1,256]{4,2,1,3,0:T(8,128)}, u32[]{:S(2)}) copy-start(f32[1,16,256,1,256]{4,2,1,3,0:T(8,128)} %copy.127) | copy-start | bytes 12582916
  455.4 10.0 %copy-start = (f32[1,16,256,1,256]{4,2,1,3,0:T(8,128)S(1)}, f32[1,16,256,1,256]{4,2,1,3,0:T(8,128)}, u32[]{:S(2)}) copy-start(f32[1,16,256,1,256]{4,2,1,3,0:T(8,128)} %copy.125) | copy-start | bytes 12582916
  455.4 10.0 %copy-start.2 = (f32[32,128,256]{2,0,1:T(8,128)S(1)}, f32[32,128,256]{2,0,1:T(8,128)}, u32[]{:S(2)}) copy-start(f32[32,128,256]{2,0,1:T(8,128)} %fusion.74) | copy-start | bytes 12582916
